TPU v7x, 32 devices: a whole 2x2x4 slice. The times are simulated.
32 devices in a mesh: ang: 8 (over z, x), tile: 4 (over y, core).
Axes of the slice: x: 2, y: 2, z: 4, core: 2. Of those that a mesh axis runs over, the one named last changes fastest.
Arguments:
- sinogram: float32 [2, 64, 2048], P(None, 'ang'), may hold values from -6 to 6
- ray_offsets: int32 [64, 256], P('ang'), may hold values from 0 to 2047
- merge_matrices: float32 [3, 2, 2, 256, 256], replicated, may hold values from -1 to 1.5, as said below
Outputs:
- reconstruction: float32 [2, 2048, 2048], P(None, 'ang')
Inputs may be any that keep to these rules, and one draw needn't show every extreme that they name: merge_matrices[l, b, k] is zero outside the columns b * (96) to b * 96 + 256 / 2 + 31.
All inputs are finite; a program needn't handle non-finite values.
Results may differ from a plain program's by a relative error of at most 0.0003.
Values sent between devices are 32-bit elements; how exact they have to be, the bound alone decides.
A program may use at most 768 MiB of HBM per device.

v0:
```python
import functools
import math

import jax
import jax.numpy as jnp
from jax import lax
from jax.experimental import pallas as pl
from jax.experimental.pallas import tpu as pltpu
from jax.sharding import PartitionSpec as P

LANES = 128
SUBLANES = 8
UNROLL = 40


def gather_kernel(groups, tiles_ref, starts_ref, all_tiles_ref, all_starts_ref, send_sems, recv_sems, own_sems):
    own = lax.axis_index("ang")
    barrier = pltpu.get_barrier_semaphore()
    for k in range(1, groups):
        pl.semaphore_signal(barrier, inc=1, device_id={"ang": own ^ k}, device_id_type=pl.DeviceIdType.MESH)
    pl.semaphore_wait(barrier, groups - 1)
    pairs = ((starts_ref, all_starts_ref), (tiles_ref, all_tiles_ref))
    copies = []
    for k in range(1, groups):
        for n, (source, target) in enumerate(pairs):
            copies.append(
                pltpu.make_async_remote_copy(
                    src_ref=source,
                    dst_ref=target.at[own],
                    send_sem=send_sems.at[n, k],
                    recv_sem=recv_sems.at[n, k],
                    device_id={"ang": own ^ k},
                    device_id_type=pl.DeviceIdType.MESH,
                )
            )
    for n, (source, target) in enumerate(pairs):
        copies.append(pltpu.make_async_copy(source, target.at[own], own_sems.at[n]))
    for copy in copies:
        copy.start()
    for copy in copies:
        copy.wait()


def gather_groups(tiles, starts, groups):
    vmem = pl.BlockSpec(memory_space=pltpu.VMEM)
    sems = pltpu.SemaphoreType.DMA((2, groups))
    return pl.pallas_call(
        functools.partial(gather_kernel, groups),
        out_shape=[jax.ShapeDtypeStruct((groups,) + x.shape, x.dtype) for x in (tiles, starts)],
        in_specs=[vmem, vmem],
        out_specs=[vmem, vmem],
        scratch_shapes=[sems, sems, pltpu.SemaphoreType.DMA((2,))],
        compiler_params=pltpu.CompilerParams(collective_id=0, has_side_effects=True),
    )(tiles, starts)


def split_bf16(value):
    high = value.astype(jnp.bfloat16)
    return high, (value - high.astype(jnp.float32)).astype(jnp.bfloat16)


def merge_kernel(dims, starts_ref, groups_ref, row0_ref, tiles_ref, weights_ref, out_ref, wide_ref, samples_ref, high_ref, low_ref):
    slices, bins, angles, rows, width, groups = dims
    per_tile = SUBLANES // slices
    count = bins // LANES // per_tile
    spread = count * (per_tile + 1)

    def widen(angle, carry):
        for i in range(count):
            tile = tiles_ref[angle * count + i]
            for u in range(spread // count):
                turn = (-slices * u) % SUBLANES
                turned = pltpu.roll(tile, turn, 0) if turn else tile
                at = (angle * spread + u * count + i) * SUBLANES
                wide_ref[pl.ds(pl.multiple_of(at, SUBLANES), SUBLANES), :] = turned
        return carry

    lax.fori_loop(0, groups * angles, widen, 0)
    reverse_lane = LANES - 1 - lax.broadcasted_iota(jnp.int32, (SUBLANES, LANES), 1)
    row0 = row0_ref[0]
    unroll = math.gcd(width, UNROLL)

    def by_group(index, carry):
        group = groups_ref[index]

        def by_rows(step, inner):
            first = (2 * rows * group + row0 + step * unroll) * angles
            for u in range(unroll):
                q = step * unroll + u
                sums = [None] * count
                for a in range(angles):
                    turn = starts_ref[first + u * angles + a + angles * rows]
                    base = starts_ref[first + u * angles + a]
                    mask = reverse_lane < turn
                    held = []
                    for i in range(count + 1):
                        at = pl.multiple_of(base + i * SUBLANES, SUBLANES)
                        held.append(wide_ref[pl.ds(at, SUBLANES), :])
                    for i in range(count):
                        moved = pltpu.roll(jnp.where(mask, held[i], held[i + 1]), turn, 1)
                        sums[i] = moved if a == 0 else sums[i] + moved
                for i in range(count):
                    at = ((index * width + q) * count + i) * SUBLANES
                    samples_ref[pl.ds(pl.multiple_of(at, SUBLANES), SUBLANES), :] = sums[i]
            return inner

        return lax.fori_loop(0, width // unroll, by_rows, carry)

    lax.fori_loop(0, groups, by_group, 0)
    high_ref[...], low_ref[...] = split_bf16(weights_ref[...])
    depth = groups * width
    pairs = bins // (2 * LANES)

    def by_columns(n, carry):
        s = n // pairs
        c0 = (n % pairs) * 2
        first = (c0 % count) * SUBLANES + (c0 // count) * slices + s
        parts = [samples_ref[pl.ds(first + k * SUBLANES, depth, stride=count * SUBLANES), :] for k in range(2)]
        field_high, field_low = split_bf16(jnp.concatenate(parts, axis=1))
        dot = functools.partial(jnp.dot, preferred_element_type=jnp.float32)
        total = dot(high_ref[...], field_high) + (dot(high_ref[...], field_low) + dot(low_ref[...], field_high))
        out_ref[s, :, pl.ds(pl.multiple_of(c0 * LANES, 2 * LANES), 2 * LANES)] = total
        return carry

    lax.fori_loop(0, slices * pairs, by_columns, 0)


def body(sinogram, ray_offsets, merge_matrices):
    slices, angles, bins = sinogram.shape
    assert slices == 2 and lax.axis_size("tile") % 2 == 0
    rows = ray_offsets.shape[1]
    margin = rows // 8
    width = rows // 2 + margin
    groups = lax.axis_size("ang")
    levels = groups.bit_length() - 1
    own = lax.axis_index("ang")
    core = lax.axis_index("tile") % slices
    per_tile = SUBLANES
    count = bins // LANES // per_tile
    spread = count * (per_tile + 1)

    own_tiles = lax.dynamic_index_in_dim(sinogram, core, 0, keepdims=False)
    own_tiles = own_tiles.reshape(angles, per_tile, count, LANES).transpose(0, 2, 1, 3)
    own_tiles = own_tiles.reshape(angles * count, SUBLANES, LANES)
    angle = own * angles + jnp.arange(angles, dtype=jnp.int32)[:, None]
    bases = (angle * spread + jnp.right_shift(ray_offsets, 7)) * SUBLANES
    turns = LANES - jnp.bitwise_and(ray_offsets, LANES - 1)
    own_starts = jnp.stack([bases, turns]).transpose(0, 2, 1).reshape(-1, LANES).astype(jnp.int32)
    tiles, starts = gather_groups(own_tiles, own_starts, groups)
    tiles = tiles.reshape(-1, SUBLANES, LANES)
    starts = starts.reshape(-1)

    bits = [jnp.right_shift(own, levels - 1 - level) & 1 for level in range(levels)]
    weights = None
    for level in range(levels - 1, -1, -1):
        matrices = lax.dynamic_index_in_dim(merge_matrices[level], bits[level], 0, keepdims=False)
        if level == 0:
            matrices = lax.dynamic_slice_in_dim(matrices, bits[0] * (rows // 2 - margin), width, 2)
        if weights is None:
            weights = matrices.transpose(1, 0, 2)
        else:
            weights = jnp.einsum("rxk,mkj->rxmj", weights, matrices, precision=lax.Precision.HIGHEST)
        weights = weights.reshape(rows, -1, matrices.shape[2])
    weights = weights.reshape(rows, groups * width) / math.sqrt(angles)

    flips = [int(format(i, f"0{levels}b")[::-1], 2) for i in range(groups)]
    group_order = jnp.bitwise_xor(own, jnp.array(flips, jnp.int32)).astype(jnp.int32)
    row0 = (bits[0] * (rows // 2 - margin)).astype(jnp.int32).reshape(1)

    smem = pl.BlockSpec(memory_space=pltpu.SMEM)
    vmem = pl.BlockSpec(memory_space=pltpu.VMEM)
    finished = pl.pallas_call(
        functools.partial(merge_kernel, (1, bins, angles, rows, width, groups)),
        out_shape=jax.ShapeDtypeStruct((1, rows, bins), jnp.float32),
        in_specs=[smem, smem, smem, vmem, vmem],
        out_specs=vmem,
        scratch_shapes=[
            pltpu.VMEM((groups * angles * spread * SUBLANES, LANES), jnp.float32),
            pltpu.VMEM((groups * width * count * SUBLANES, LANES), jnp.float32),
            pltpu.VMEM((rows, groups * width), jnp.bfloat16),
            pltpu.VMEM((rows, groups * width), jnp.bfloat16),
        ],
        compiler_params=pltpu.CompilerParams(vmem_limit_bytes=60 * 1024 * 1024),
    )(starts, group_order, row0, tiles, weights)
    swaps = [(i, i ^ 1) for i in range(lax.axis_size("tile"))]
    other = lax.ppermute(finished, "tile", swaps)
    place = lax.broadcasted_iota(jnp.int32, (slices, 1, 1), 0)
    return jnp.where(place == core, finished, other)


def solution(mesh):
    placed = (P(None, "ang", None), P("ang", None), P())
    return jax.shard_map(
        body, mesh=mesh, in_specs=placed, out_specs=P(None, "ang", None), check_vma=False
    )
```

profile of v0, /device:TPU:0, one launch (start us, length us, event | category | flops | bytes accessed | tf_op | source)
XLA Modules:
  0.0 76.0 jit_solution(2242580719187695263)
XLA Ops:
  0.0 0.0 copy-start
  0.0 1.2 %broadcast_xor_fusion.groups_ref = s32[8]{0:T(128)} fusion(s32[8]{0:T(128)} %constant.83.clone, s32[]{:T(128)S(6)} %axis_index.25), kind=kLoop, calls=%fused_computation.17 | loop fusion | flops 8 | bytes 68 | tf_op jit(solution)/shard_map/xor | solution.py:167
  1.2 0.0 copy-done
  1.2 0.1 reshape.43
  1.3 0.6 copy.8
  1.9 0.8 %multiply_bitcast_fusion = (s32[1,8,256]{2,1,0:T(8,128)S(1)}, s32[1,8,256]{2,1,0:T(8,128)S(1)}) fusion(s32[8,256]{1,0:T(8,128)} %param.5, s32[8]{0:T(128)S(1)} %add_multiply_fusion), kind=kLoop, calls=%fused_computation.11 | loop fusion | flops 10240 | bytes 24608 | tf_op jit(solution)/shard_map/stack | solution.py:148
  2.7 0.1 copy.9
  2.8 0.7 reshape.45.starts_ref
  3.6 2.2 %fusion.9 = (f32[1,2,2,256,256]{4,3,2,1,0:T(8,128)S(1)}, f32[1,2,2,256,256]{4,3,2,1,0:T(8,128)S(1)}, f32[1,2,2,256,256]{4,3,2,1,0:T(8,128)S(1)}) fusion(f32[3,2,2,256,256]{4,3,2,1,0:T(8,128)} %param.6), kind=kLoop, calls=%fused_computation.18 | loop fusion | bytes 6291456 | tf_op jit(solution)/shard_map/slice | solution.py:156
  5.8 1.0 %fusion.1 = f32[256,2,2,256]{3,0,2,1:T(8,128)S(1)} fusion(f32[1,2,2,256,256]{4,3,2,1,0:T(8,128)S(1)} %get-tuple-element.11, s32[]{:T(128)S(6)} %select_n.35, f32[1,2,2,256,256]{4,3,2,1,0:T(8,128)S(1)} %get-tuple-element.10, s32[]{:T(128)S(6)} %select_n.34), kind=kOutput, calls=%fused_computation.3 | convolution fusion | flops 805306368 | bytes 2097160 | tf_op jit(solution)/shard_map/rxk,mkj->rxmj/dot_general | solution.py:162
  6.8 1.5 %convolution_multiply_fusion = f32[256,4,2,160]{0,3,2,1:T(8,128)S(1)} fusion(f32[256,4,256,1]{2,0,3,1:T(8,128)S(1)} %bitcast.42, f32[1,2,2,256,256]{4,3,2,1,0:T(8,128)S(1)} %get-tuple-element.9, s32[]{:T(128)S(6)} %select_n.37, s32[]{:T(128)S(6)} %select_n.39), kind=kOutput, calls=%fused_computation.1 | convolution fusion | flops 1006960640 | bytes 2883592 | tf_op jit(solution)/shard_map/rxk,mkj->rxmj/dot_general | solution.py:162
  8.3 1.5 %copy.11.weights_ref = f32[256,1280]{1,0:T(8,128)} copy(f32[256,1280]{0,1:T(8,128)S(1)} %bitcast.41) | data formatting | bytes 2621440 | tf_op jit(solution)/shard_map/div | solution.py:164
  9.8 20.7 %shard_map.46 = (f32[8,16,8,128]{3,2,1,0:T(8,128)}, s32[8,32,128]{2,1,0:T(8,128)}) custom-call(f32[16,8,128]{2,1,0:T(8,128)} %bitcast.45, s32[32,128]{1,0:T(8,128)} %reshape.45.starts_ref), custom_call_target="tpu_custom_call" | custom-call | tf_op jit(solution)/shard_map/pallas_call | solution.py:47
  30.4 36.8 %shard_map.47 = f32[1,256,2048]{2,1,0:T(8,128)} custom-call(s32[32768]{0:T(1024)} %bitcast.47, s32[8]{0:T(128)} %broadcast_xor_fusion.groups_ref, s32[1]{0:T(128)} %bitcast.6.row0_ref, f32[128,8,128]{2,1,0:T(8,128)} %bitcast.44, f32[256,1280]{1,0:T(8,128)} %copy.11.weights_ref), custom_call_target="tpu_custom_call" | custom-call | tf_op jit(solution)/shard_map/pallas_call | solution.py:172
  67.3 0.0 collective-permute-start
  67.3 4.4 %collective-permute-done = f32[1,256,2048]{2,1,0:T(8,128)S(1)} collective-permute-done((f32[1,256,2048]{2,1,0:T(8,128)}, f32[1,256,2048]{2,1,0:T(8,128)S(1)}, u32[]{:S(2)}, u32[]{:S(2)}) %collective-permute-start) | collective-permute-done | bytes 2097184 | tf_op jit(solution)/shard_map/ppermute | solution.py:186
  71.7 4.3 %broadcast_select_fusion = f32[2,256,2048]{2,1,0:T(8,128)} fusion(f32[256,2048]{1,0:T(8,128)S(1)} %bitcast.43, f32[256,2048]{1,0:T(8,128)} %bitcast.40, pred[2]{0:T(512)(128)(4,1)S(1)} %iota_compare_fusion), kind=kLoop, calls=%fused_computation | loop fusion | flops 1048576 | bytes 8388610 | tf_op jit(solution)/shard_map/jit(_where)/select_n | solution.py:188
  (4 shorter events, 0.0 us)
Async XLA Ops:
  0.0 1.2 %copy-start = (f32[2,8,2048]{2,1,0:T(8,128)S(1)}, f32[2,8,2048]{2,1,0:T(8,128)}, u32[]{:S(2)}) copy-start(f32[2,8,2048]{2,1,0:T(8,128)} %param.4) | copy-start | bytes 393220
  67.3 4.4 %collective-permute-start = (f32[1,256,2048]{2,1,0:T(8,128)}, f32[1,256,2048]{2,1,0:T(8,128)S(1)}, u32[]{:S(2)}, u32[]{:S(2)}) collective-permute-start(f32[1,256,2048]{2,1,0:T(8,128)} %shard_map.47), channel_id=1, source_target_pairs={{0,1},{1,0},{2,3},{3,2},{4,5},{5,4},{6,7},{7,6},{8,9},{9,8},{10,11... | collective-permute-start | bytes 6291464 | tf_op jit(solution)/shard_map/ppermute | solution.py:186
where the time goes:
time: 76.5 us; the launch traced here: 76 us
  Pallas kernels  57.5 us (75%)
  other arithmetic  6.3 us (8%)
  local copies, waits for them, and re-layouts  5.27 us (7%)
  waiting for transfers between devices  4.36 us (6%)
  matrix products  2.48 us (3%)
    pallas_call x1, Pallas kernels, body(): pl.pallas_call(functools.partial(merge_kernel, (1, bins, angles, rows, wi...  36.8 us
    pallas_call x1, Pallas kernels, gather_groups(): pl.pallas_call(functools.partial(gather_kernel, groups), out_shape=[jax.S...  20.7 us
    ppermute x1, waiting for transfers between devices, body(): other = lax.ppermute(finished, 'tile', swaps)  4.36 us
    select_n x1, other arithmetic, body(): return jnp.where(place == core, finished, other)  4.32 us
    dot_general x2, matrix products, body(): jnp.einsum('rxk,mkj->rxmj', weights, matrices, precision=lax.Precision.HI...  2.48 us
    slice x1, local copies, waits for them, and re-layouts, body(): merge_matrices[level]  2.23 us
  transfers between devices with their start and end apart: 1, of which 1 were waited for; matrix products, arithmetic and copies ran while one was open for 0% of the time, Pallas kernels for 0%

commit v1 on v0

v1 whole, which is shorter than its diff:
```python
import functools
import math

import jax
import jax.numpy as jnp
from jax import lax
from jax.experimental import pallas as pl
from jax.experimental.pallas import tpu as pltpu
from jax.sharding import PartitionSpec as P

LANES = 128
SUBLANES = 8
PITCH = 3 * SUBLANES + 1
ROW_PITCH = SUBLANES + 1
UNROLL = 80
TOP = 32767.0


def split_bf16(value):
    high = value.astype(jnp.bfloat16)
    return high, (value - high.astype(jnp.float32)).astype(jnp.bfloat16)


def dot3(left, right):
    dot = functools.partial(jnp.dot, preferred_element_type=jnp.float32)
    return dot(left[0], right[0]) + (dot(left[0], right[1]) + dot(left[1], right[0]))


def fused_kernel(dims, sino_ref, offsets_ref, merge_ref, out_ref, field_in, index_in, index_smem, merges, table_ref, samples_ref,
                 weights_high, weights_low, in_sems, smem_sems, send_sems, recv_sems, swap_send, swap_recv):
    levels, angles, rows, bins = dims
    groups = 2**levels
    margin = rows // 8
    width = rows // 2 + margin
    half = bins // 2
    own = lax.axis_index("ang")
    seat = lax.axis_index("tile")
    core = lax.rem(seat, 2)
    bits = [lax.rem(lax.div(own, 2 ** (levels - 1 - level)), 2) for level in range(levels)]

    loads = [pltpu.make_async_copy(sino_ref.at[core], field_in.at[0, :, pl.ds(0, bins)], in_sems.at[0])]
    for level in range(levels):
        loads.append(pltpu.make_async_copy(merge_ref.at[level, bits[level]], merges.at[level], in_sems.at[1 + level]))
    for load in loads:
        load.start()

    barrier = pltpu.get_barrier_semaphore()
    far = list(range(2, groups, 2))
    peers = [{"ang": own ^ k} for k in [1] + far] + [{"tile": seat ^ 1}]
    for peer in peers:
        pl.semaphore_signal(barrier, inc=1, device_id=peer, device_id_type=pl.DeviceIdType.MESH)

    index_in[0] = jnp.bitwise_and(offsets_ref[...] + (bins - 1), bins - 1) ^ (LANES - 1)
    loads[0].wait()
    largest = jnp.max(jnp.abs(field_in[0, :, pl.ds(0, bins)]))
    field_in[0, :, pl.ds(bins, LANES)] = jnp.full((angles, LANES), 1.0, jnp.float32) * largest
    pl.semaphore_wait(barrier, len(peers))

    def sends(k, target, slot):
        return [
            pltpu.make_async_remote_copy(
                src_ref=buffer.at[k],
                dst_ref=buffer.at[slot],
                send_sem=send_sems.at[n, slot],
                recv_sem=recv_sems.at[n, slot],
                device_id={"ang": target},
                device_id_type=pl.DeviceIdType.MESH,
            )
            for n, buffer in enumerate((field_in, index_in))
        ]

    moves = {k: sends(0, own ^ k, k) for k in [1] + far}
    for k in [1] + far:
        for move in moves[k]:
            move.start()
    index_copy = pltpu.make_async_copy(index_in.at[0], index_smem.at[0], smem_sems.at[0])
    index_copy.start()

    def prepare(k):
        peak = field_in[k, :, pl.ds(bins, LANES)]
        scale = TOP / jnp.maximum(peak, 1e-30)
        blocks = bins // LANES
        coded = []
        for block in range(blocks):
            value = field_in[k, :, pl.ds(block * LANES, LANES)]
            coded.append((value * scale + (TOP + 1.5)).astype(jnp.int32))
        for block in range(blocks):
            upper = jnp.left_shift(coded[(block + blocks // 2) % blocks] - int(TOP + 1), 16)
            packed = jnp.bitwise_or(upper, coded[block])
            for place in (block, block + blocks):
                if place < PITCH - 1:
                    table_ref[pl.ds(k * angles * PITCH + place, angles, stride=PITCH), :] = packed

    reverse_lane = LANES - 1 - lax.broadcasted_iota(jnp.int32, (SUBLANES, LANES), 1)
    row0 = bits[0] * (rows // 2 - margin)
    unroll = math.gcd(width, UNROLL)
    samples_half = groups * width * ROW_PITCH

    def project(k):
        unit = field_in[k, :, pl.ds(bins, LANES)] * (1.0 / (TOP * math.sqrt(angles)))

        def by_rows(step, carry):
            for u in range(unroll):
                q = step * unroll + u
                total = None
                upper = None
                for a in range(angles):
                    code = index_smem[k, a, row0 + q]
                    turn = jnp.bitwise_and(code, LANES - 1)
                    base = jnp.right_shift(code, 7) + (k * angles + a) * PITCH
                    near = table_ref[pl.ds(base, SUBLANES), :]
                    next_ = table_ref[pl.ds(base + 1, SUBLANES), :]
                    moved = pltpu.roll(jnp.where(reverse_lane < turn, near, next_), turn, 1)
                    high = jnp.right_shift(moved, 16)
                    total = moved if a == 0 else total + moved
                    upper = high if a == 0 else upper + high
                lower = total - jnp.left_shift(upper, 16) - angles * int(TOP + 1)
                at = (k * width + q) * ROW_PITCH
                samples_ref[pl.ds(at, SUBLANES), :] = lower.astype(jnp.float32) * unit
                samples_ref[pl.ds(samples_half + at, SUBLANES), :] = upper.astype(jnp.float32) * unit
            return carry

        lax.fori_loop(0, width // unroll, by_rows, 0)

    def prepare_weights():
        for load in loads[1:]:
            load.wait()
        parts = None
        for level in range(levels - 1, -1, -1):
            matrices = [merges[level, m] for m in range(2)]
            if level == 0:
                matrices = [jnp.where(bits[0] == 1, m[:, rows - width:], m[:, :width]) for m in matrices]
            if parts is None:
                parts = matrices
            else:
                matrices = [split_bf16(m) for m in matrices]
                parts = [dot3(part, m) for part in [split_bf16(p) for p in parts] for m in matrices]
        flips = [int(format(k, f"0{levels}b")[::-1], 2) for k in range(groups)]
        whole = jnp.concatenate([parts[i] for i in flips], axis=1)
        weights_high[...], weights_low[...] = split_bf16(whole)

    prepare(0)
    index_copy.wait()
    project(0)
    prepare_weights()
    forwards = {}
    for k in [1] + far + [f ^ 1 for f in far]:
        arrived = moves[k] if k in moves else forwards[k]
        for move in arrived:
            move.wait_recv()
        if k in far:
            forwards[k ^ 1] = sends(k, own ^ 1, k ^ 1)
            for move in forwards[k ^ 1]:
                move.start()
        index_copy = pltpu.make_async_copy(index_in.at[k], index_smem.at[k], smem_sems.at[k])
        index_copy.start()
        prepare(k)
        index_copy.wait()
        project(k)

    depth = groups * width
    pairs = bins // (2 * LANES)

    def swap(n):
        at = pl.ds(pl.multiple_of(n * 2 * LANES, 2 * LANES), 2 * LANES)
        return pltpu.make_async_remote_copy(
            src_ref=out_ref.at[core, :, at],
            dst_ref=out_ref.at[core, :, at],
            send_sem=swap_send.at[n],
            recv_sem=swap_recv.at[n],
            device_id={"tile": seat ^ 1},
            device_id_type=pl.DeviceIdType.MESH,
        )

    def by_columns(n, carry):
        first = (n // (pairs // 2)) * samples_half + (n % (pairs // 2)) * 2
        parts = [samples_ref[pl.ds(first + i, depth, stride=ROW_PITCH), :] for i in range(2)]
        field = split_bf16(jnp.concatenate(parts, axis=1))
        total = dot3((weights_high[...], weights_low[...]), field)
        out_ref[core, :, pl.ds(pl.multiple_of(n * 2 * LANES, 2 * LANES), 2 * LANES)] = total

        @pl.when(n > 0)
        def _():
            swap(n - 1).start()

        return carry

    lax.fori_loop(0, pairs, by_columns, 0)
    swap(pairs - 1).start()
    for k in moves:
        for move in moves[k]:
            move.wait_send()
    for k in forwards:
        for move in forwards[k]:
            move.wait_send()
    for n in range(pairs):
        swap(n).wait()


def body(sinogram, ray_offsets, merge_matrices):
    slices, angles, bins = sinogram.shape
    rows = ray_offsets.shape[1]
    levels = merge_matrices.shape[0]
    groups = lax.axis_size("ang")
    assert slices == 2 and lax.axis_size("tile") % 2 == 0
    assert groups == 2**levels and angles == SUBLANES and bins == 2 * SUBLANES * LANES
    width = rows // 2 + rows // 8
    vmem = pl.BlockSpec(memory_space=pltpu.VMEM)
    anywhere = pl.BlockSpec(memory_space=pl.ANY)
    dma = pltpu.SemaphoreType.DMA
    return pl.pallas_call(
        functools.partial(fused_kernel, (levels, angles, rows, bins)),
        out_shape=jax.ShapeDtypeStruct((slices, rows, bins), jnp.float32),
        in_specs=[anywhere, vmem, anywhere],
        out_specs=vmem,
        scratch_shapes=[
            pltpu.VMEM((groups, angles, bins + LANES), jnp.float32),
            pltpu.VMEM((groups, angles, rows), jnp.int32),
            pltpu.SMEM((groups, angles, rows), jnp.int32),
            pltpu.VMEM((levels, 2, rows, rows), jnp.float32),
            pltpu.VMEM((groups * angles * PITCH, LANES), jnp.int32),
            pltpu.VMEM((2 * groups * width * ROW_PITCH, LANES), jnp.float32),
            pltpu.VMEM((rows, groups * width), jnp.bfloat16),
            pltpu.VMEM((rows, groups * width), jnp.bfloat16),
            dma((1 + levels,)),
            dma((groups,)),
            dma((2, groups)),
            dma((2, groups)),
            dma((bins // (2 * LANES),)),
            dma((bins // (2 * LANES),)),
        ],
        compiler_params=pltpu.CompilerParams(
            collective_id=0, has_side_effects=True, vmem_limit_bytes=48 * 1024 * 1024
        ),
    )(sinogram, ray_offsets, merge_matrices)


def solution(mesh):
    placed = (P(None, "ang", None), P("ang", None), P())
    return jax.shard_map(
        body, mesh=mesh, in_specs=placed, out_specs=P(None, "ang", None), check_vma=False
    )
```

time: 76.5 us -> 49.4 us (0.65)
  Pallas kernels: 57.5 us -> 41 us
  other arithmetic: 6.3 us -> 0 us
  waiting for transfers between devices: 4.36 us -> 0 us
  local copies, waits for them, and re-layouts: 5.27 us -> 8.19 us
  matrix products: 2.48 us -> 0 us
    pallas_call x2 -> x1, Pallas kernels: 57.5 us -> 41 us  [body(): pl.pallas_call(functools.partial(fused_kernel, (levels, angles, rows, bin...]
    unnamed x2 -> x7, local copies, waits for them, and re-layouts: 0.01 us -> 8.19 us
    ppermute x1 -> x0, waiting for transfers between devices: 4.36 us -> none  [body(): other = lax.ppermute(finished, 'tile', swaps)]
    select_n x1 -> x0, other arithmetic: 4.32 us -> none  [body(): return jnp.where(place == core, finished, other)]
    dot_general x2 -> x0, matrix products: 2.48 us -> none  [body(): jnp.einsum('rxk,mkj->rxmj', weights, matrices, precision=lax.Precision.HI...]
    slice x1 -> x0, local copies, waits for them, and re-layouts: 2.23 us -> none  [body(): merge_matrices[level]]
    div x1 -> x0, local copies, waits for them, and re-layouts: 1.46 us -> none  [body(): weights = weights.reshape(rows, groups * width) / math.sqrt(angles)]
    xor x1 -> x0, other arithmetic: 1.19 us -> none  [body(): jnp.bitwise_xor(own, jnp.array(flips, jnp.int32)).astype(jnp.int32)]
  transfers between devices with their start and end apart: 1 -> 0, of which waited for: 1 -> 0; matrix products, arithmetic and copies ran while one was open for 0% -> 0% of each run, Pallas kernels for 0% -> 0%
where the time goes in v1:
time: 49.4 us; the launch traced here: 49.2 us
  Pallas kernels  41 us (83%)
  local copies, waits for them, and re-layouts  8.19 us (17%)
    pallas_call x1, Pallas kernels, body(): pl.pallas_call(functools.partial(fused_kernel, (levels, angles, rows, bin...  41 us
    unnamed x7, local copies, waits for them, and re-layouts  8.19 us

profile of v1, /device:TPU:0, one launch (start us, length us, event | category | flops | bytes accessed | tf_op | source)
XLA Modules:
  0.0 49.2 jit_solution(505901062937631802)
XLA Ops:
  0.0 0.0 copy-start
  0.0 1.9 %copy-done = f32[3,2,2,256,256]{4,3,2,1,0:T(8,128)S(1)} copy-done((f32[3,2,2,256,256]{4,3,2,1,0:T(8,128)S(1)}, f32[3,2,2,256,256]{4,3,2,1,0:T(8,128)}, u32[]{:S(2)}) %copy-start) | copy-done | bytes 3145752
  1.9 0.0 copy-start.1
  1.9 0.9 %copy-done.1 = f32[2,8,2048]{2,1,0:T(8,128)S(1)} copy-done((f32[2,8,2048]{2,1,0:T(8,128)S(1)}, f32[2,8,2048]{2,1,0:T(8,128)}, u32[]{:S(2)}) %copy-start.1) | copy-done | bytes 131096
  2.8 0.0 copy-start.2
  2.8 0.7 %copy-done.2 = s32[8,256]{1,0:T(8,128)S(1)} copy-done((s32[8,256]{1,0:T(8,128)S(1)}, s32[8,256]{1,0:T(8,128)}, u32[]{:S(2)}) %copy-start.2) | copy-done | bytes 8216
  3.5 41.0 %shard_map.37 = f32[2,256,2048]{2,1,0:T(8,128)} custom-call(f32[2,8,2048]{2,1,0:T(8,128)S(1)} %copy-done.1, s32[8,256]{1,0:T(8,128)S(1)} %copy-done.2, f32[3,2,2,256,256]{4,3,2,1,0:T(8,128)S(1)} %copy-done), custom_call_target="tpu_custom_call" | custom-call | tf_op jit(solution)/shard_map/pallas_call | solution.py:211
  44.5 4.7 %copy.5 = f32[2,256,2048]{2,1,0:T(8,128)} copy(f32[2,256,2048]{2,1,0:T(8,128)} %shard_map.37) | data formatting | bytes 8388608
Async XLA Ops:
  0.0 1.9 %copy-start = (f32[3,2,2,256,256]{4,3,2,1,0:T(8,128)S(1)}, f32[3,2,2,256,256]{4,3,2,1,0:T(8,128)}, u32[]{:S(2)}) copy-start(f32[3,2,2,256,256]{4,3,2,1,0:T(8,128)} %merge_ref.1) | copy-start | bytes 9437188
  1.9 0.9 %copy-start.1 = (f32[2,8,2048]{2,1,0:T(8,128)S(1)}, f32[2,8,2048]{2,1,0:T(8,128)}, u32[]{:S(2)}) copy-start(f32[2,8,2048]{2,1,0:T(8,128)} %sino_ref.1) | copy-start | bytes 393220
  2.8 0.7 %copy-start.2 = (s32[8,256]{1,0:T(8,128)S(1)}, s32[8,256]{1,0:T(8,128)}, u32[]{:S(2)}) copy-start(s32[8,256]{1,0:T(8,128)} %offsets_ref.1) | copy-start | bytes 24580

commit v2 on v1

v2 whole, which is shorter than its diff:
```python
import functools
import math

import jax
import jax.numpy as jnp
from jax import lax
from jax.experimental import pallas as pl
from jax.experimental.pallas import tpu as pltpu
from jax.sharding import PartitionSpec as P

LANES = 128
SUBLANES = 8
PITCH = 3 * SUBLANES + 1
ROW_PITCH = SUBLANES + 1
TOP = 32767.0


def split_bf16(value):
    high = value.astype(jnp.bfloat16)
    return high, (value - high.astype(jnp.float32)).astype(jnp.bfloat16)


def dot3(left, right):
    dot = functools.partial(jnp.dot, preferred_element_type=jnp.float32)
    return dot(left[0], right[0]) + (dot(left[0], right[1]) + dot(left[1], right[0]))


def fused_kernel(dims, sino_ref, offsets_ref, merge_ref, out_ref, field_in, index_in, index_kept, index_smem, merges, table_ref, samples_ref,
                 weights_high, weights_low, in_sems, smem_sems, send_sems, recv_sems, swap_send, swap_recv):
    levels, angles, rows, bins = dims
    groups = 2**levels
    width = rows // 2 + rows // 8
    half = bins // 2
    own = lax.axis_index("ang")
    seat = lax.axis_index("tile")
    core = lax.rem(seat, 2)
    bits = [lax.rem(lax.div(own, 2 ** (levels - 1 - level)), 2) for level in range(levels)]

    loads = [pltpu.make_async_copy(sino_ref.at[core], field_in.at[0, :, pl.ds(0, bins)], in_sems.at[0])]
    for level in range(levels):
        loads.append(pltpu.make_async_copy(merge_ref.at[level, bits[level]], merges.at[level], in_sems.at[1 + level]))
    for load in loads:
        load.start()

    barrier = pltpu.get_barrier_semaphore()
    far = list(range(2, groups, 2))
    peers = [{"ang": own ^ k} for k in [1] + far] + [{"tile": seat ^ 1}]
    for peer in peers:
        pl.semaphore_signal(barrier, inc=1, device_id=peer, device_id_type=pl.DeviceIdType.MESH)

    index_in[0] = jnp.bitwise_and(offsets_ref[...] + (bins - 1), bins - 1) ^ (LANES - 1)
    loads[0].wait()
    largest = jnp.max(jnp.abs(field_in[0, :, pl.ds(0, bins)]))
    field_in[0, :, pl.ds(bins, LANES)] = jnp.full((angles, LANES), 1.0, jnp.float32) * largest
    pl.semaphore_wait(barrier, len(peers))

    def send(n, k, target, slot):
        buffer = (index_in, field_in)[n]
        return pltpu.make_async_remote_copy(
            src_ref=buffer.at[k],
            dst_ref=buffer.at[slot],
            send_sem=send_sems.at[n, slot],
            recv_sem=recv_sems.at[n, slot],
            device_id={"ang": target},
            device_id_type=pl.DeviceIdType.MESH,
        )

    for n in range(2):
        for k in [1] + far:
            send(n, 0, own ^ k, k).start()

    turn_point = groups // 2

    def group_at(place):
        near = jnp.where(place <= turn_point, 2 * place - 2, 2 * (place - turn_point) + 1)
        return jnp.where(place < 2, place, near)

    def receive(n, place):
        k = group_at(place)

        @pl.when(place > 0)
        def _():
            send(n, k, own, k).wait_recv()

        @pl.when(jnp.logical_and(place >= 2, place <= turn_point))
        def _():
            send(n, k, own ^ 1, k + 1).start()

        return k

    def hand_over(place, side):
        codes = index_in[receive(0, place)]
        codes = jnp.where(bits[0] == 1, codes[:, rows - width:], codes[:, :width])
        index_kept[side] = codes + lax.broadcasted_iota(jnp.int32, codes.shape, 0) * (PITCH * LANES)
        index_copy(side).start()

    def index_copy(side):
        return pltpu.make_async_copy(index_kept.at[side], index_smem.at[side], smem_sems.at[side])

    def prepare(place, side):
        k = receive(1, place)
        peak = field_in[k, :, pl.ds(bins, LANES)]
        scale = TOP / jnp.maximum(peak, 1e-30)
        blocks = bins // LANES
        coded = []
        for block in range(blocks):
            value = field_in[k, :, pl.ds(block * LANES, LANES)]
            coded.append((value * scale + (TOP + 1.5)).astype(jnp.int32))
        for block in range(blocks):
            upper = jnp.left_shift(coded[(block + blocks // 2) % blocks] - int(TOP + 1), 16)
            packed = jnp.bitwise_or(upper, coded[block])
            for at in (block, block + blocks):
                if at < PITCH - 1:
                    table_ref[side, pl.ds(at, angles, stride=PITCH), :] = packed
        return peak * (1.0 / (TOP * math.sqrt(angles)))

    reverse_lane = LANES - 1 - lax.broadcasted_iota(jnp.int32, (SUBLANES, LANES), 1)
    samples_half = groups * width * ROW_PITCH

    def project(place, side, unit):
        start = place * (width * ROW_PITCH)
        for q in range(width):
            total = None
            upper = None
            for a in range(angles):
                code = index_smem[side, a, q]
                turn = jnp.bitwise_and(code, LANES - 1)
                base = jnp.right_shift(code, 7)
                near = table_ref[side, pl.ds(base, SUBLANES), :]
                next_ = table_ref[side, pl.ds(base + 1, SUBLANES), :]
                moved = pltpu.roll(jnp.where(reverse_lane < turn, near, next_), turn, 1)
                high = jnp.right_shift(moved, 16)
                total = moved if a == 0 else total + moved
                upper = high if a == 0 else upper + high
            lower = total - jnp.left_shift(upper, 16) - angles * int(TOP + 1)
            at = start + q * ROW_PITCH
            samples_ref[0, pl.ds(at, SUBLANES), :] = lower.astype(jnp.float32) * unit
            samples_ref[1, pl.ds(at, SUBLANES), :] = upper.astype(jnp.float32) * unit

    def prepare_weights():
        for load in loads[1:]:
            load.wait()
        parts = None
        for level in range(levels - 1, -1, -1):
            matrices = [merges[level, m] for m in range(2)]
            if level == 0:
                matrices = [jnp.where(bits[0] == 1, m[:, rows - width:], m[:, :width]) for m in matrices]
            if parts is None:
                parts = matrices
            else:
                matrices = [split_bf16(m) for m in matrices]
                parts = [dot3(part, m) for part in [split_bf16(p) for p in parts] for m in matrices]
        order = [0, 1] + far + [k ^ 1 for k in far]
        flips = [int(format(k, f"0{levels}b")[::-1], 2) for k in order]
        whole = jnp.concatenate([parts[i] for i in flips], axis=1)
        weights_high[...], weights_low[...] = split_bf16(whole)

    hand_over(0, 0)
    prepare_weights()

    def by_pairs(step, carry):
        place = 2 * step
        hand_over(place + 1, 1)
        unit = prepare(place, 0)
        index_copy(0).wait()
        project(place, 0, unit)

        @pl.when(place + 2 < groups)
        def _():
            hand_over(place + 2, 0)

        unit = prepare(place + 1, 1)
        index_copy(1).wait()
        project(place + 1, 1, unit)
        return carry

    lax.fori_loop(0, groups // 2, by_pairs, 0)

    depth = groups * width
    pairs = bins // (2 * LANES)

    def swap(n):
        at = pl.ds(pl.multiple_of(n * 2 * LANES, 2 * LANES), 2 * LANES)
        return pltpu.make_async_remote_copy(
            src_ref=out_ref.at[core, :, at],
            dst_ref=out_ref.at[core, :, at],
            send_sem=swap_send.at[n],
            recv_sem=swap_recv.at[n],
            device_id={"tile": seat ^ 1},
            device_id_type=pl.DeviceIdType.MESH,
        )

    def by_columns(n, carry):
        side = n // (pairs // 2)
        first = (n % (pairs // 2)) * 2
        parts = [samples_ref[side, pl.ds(first + i, depth, stride=ROW_PITCH), :] for i in range(2)]
        field = split_bf16(jnp.concatenate(parts, axis=1))
        total = dot3((weights_high[...], weights_low[...]), field)
        out_ref[core, :, pl.ds(pl.multiple_of(n * 2 * LANES, 2 * LANES), 2 * LANES)] = total

        @pl.when(n > 0)
        def _():
            swap(n - 1).start()

        return carry

    lax.fori_loop(0, pairs, by_columns, 0)
    swap(pairs - 1).start()
    for n in range(2):
        for k in range(1, groups):
            send(n, 0, own, k).wait_send()
    for n in range(pairs):
        swap(n).wait()


def body(sinogram, ray_offsets, merge_matrices):
    slices, angles, bins = sinogram.shape
    rows = ray_offsets.shape[1]
    levels = merge_matrices.shape[0]
    groups = lax.axis_size("ang")
    assert slices == 2 and lax.axis_size("tile") % 2 == 0
    assert groups == 2**levels and angles == SUBLANES and bins == 2 * SUBLANES * LANES
    width = rows // 2 + rows // 8
    vmem = pl.BlockSpec(memory_space=pltpu.VMEM)
    hbm = pl.BlockSpec(memory_space=pltpu.HBM)
    dma = pltpu.SemaphoreType.DMA
    return pl.pallas_call(
        functools.partial(fused_kernel, (levels, angles, rows, bins)),
        out_shape=pltpu.VMEM((slices, rows, bins), jnp.float32),
        in_specs=[hbm, vmem, hbm],
        out_specs=vmem,
        scratch_shapes=[
            pltpu.VMEM((groups, angles, bins + LANES), jnp.float32),
            pltpu.VMEM((groups, angles, rows), jnp.int32),
            pltpu.VMEM((2, angles, width), jnp.int32),
            pltpu.SMEM((2, angles, width), jnp.int32),
            pltpu.VMEM((levels, 2, rows, rows), jnp.float32),
            pltpu.VMEM((2, angles * PITCH, LANES), jnp.int32),
            pltpu.VMEM((2, groups * width * ROW_PITCH + SUBLANES, LANES), jnp.float32),
            pltpu.VMEM((rows, groups * width), jnp.bfloat16),
            pltpu.VMEM((rows, groups * width), jnp.bfloat16),
            dma((1 + levels,)),
            dma((2,)),
            dma((2, groups)),
            dma((2, groups)),
            dma((bins // (2 * LANES),)),
            dma((bins // (2 * LANES),)),
        ],
        compiler_params=pltpu.CompilerParams(
            collective_id=0, has_side_effects=True, vmem_limit_bytes=48 * 1024 * 1024
        ),
    )(*[pltpu.with_memory_space_constraint(x, pltpu.HBM) for x in (sinogram, ray_offsets, merge_matrices)])


def solution(mesh):
    placed = (P(None, "ang", None), P("ang", None), P())
    return jax.shard_map(
        body, mesh=mesh, in_specs=placed, out_specs=P(None, "ang", None), check_vma=False
    )
```

time: 49.4 us -> 32.1 us (0.65)
  Pallas kernels: 41 us -> 29.9 us
  local copies, waits for them, and re-layouts: 8.19 us -> 2.02 us
    pallas_call x1, Pallas kernels: 41 us -> 29.9 us  [body(): pl.pallas_call(functools.partial(fused_kernel, (levels, angles, rows, bin...]
    unnamed x7 -> x1, local copies, waits for them, and re-layouts: 8.19 us -> 2.02 us
where the time goes in v2:
time: 32.1 us; the launch traced here: 31.9 us
  Pallas kernels  29.9 us (93%)
  local copies, waits for them, and re-layouts  2.02 us (6%)
    pallas_call x1, Pallas kernels, body(): pl.pallas_call(functools.partial(fused_kernel, (levels, angles, rows, bin...  29.9 us
    unnamed x1, local copies, waits for them, and re-layouts  2.02 us

profile of v2, /device:TPU:0, one launch (start us, length us, event | category | flops | bytes accessed | tf_op | source)
XLA Modules:
  0.0 31.9 jit_solution(7287025178109918565)
XLA Ops:
  0.0 29.9 %shard_map.37 = f32[2,256,2048]{2,1,0:T(8,128)S(1)} custom-call(f32[2,8,2048]{2,1,0:T(8,128)} %sino_ref.1, s32[8,256]{1,0:T(8,128)} %offsets_ref.1, f32[3,2,2,256,256]{4,3,2,1,0:T(8,128)} %merge_ref.1), custom_call_target="tpu_custom_call" | custom-call | tf_op jit(solution)/shard_map/pallas_call | solution.py:227
  29.9 2.0 %copy.5 = f32[2,256,2048]{2,1,0:T(8,128)} copy(f32[2,256,2048]{2,1,0:T(8,128)S(1)} %shard_map.37) | data formatting | bytes 8388608

commit v3 on v2

v3 whole, which is shorter than its diff:
```python
import functools
import math

import jax
import jax.numpy as jnp
from jax import lax
from jax.experimental import pallas as pl
from jax.experimental.pallas import tpu as pltpu
from jax.sharding import PartitionSpec as P

LANES = 128
SUBLANES = 8
PITCH = 3 * SUBLANES + 1
ROW_PITCH = SUBLANES + 4
TOP = 32767.0


def split_bf16(value):
    high = value.astype(jnp.bfloat16)
    return high, (value - high.astype(jnp.float32)).astype(jnp.bfloat16)


def dot3(left, right):
    dot = functools.partial(jnp.dot, preferred_element_type=jnp.float32)
    return dot(left[0], right[0]) + (dot(left[0], right[1]) + dot(left[1], right[0]))


def fused_kernel(dims, sino_ref, offsets_ref, merge_ref, out_ref, field_in, index_in, index_smem, offsets, merges, table_ref,
                 samples_ref, weights_high, weights_low, in_sems, smem_sems, send_sems, recv_sems, ready_sem, swap_send, swap_recv):
    levels, angles, rows, bins = dims
    groups = 2**levels
    lines = groups // 2
    cuts = (rows // 2 - rows // 8, rows // 2 + rows // 8)
    width = cuts[1]
    own = lax.axis_index("ang")
    line, column = lax.div(own, 2), lax.rem(own, 2)
    seat = lax.axis_index("tile")
    core = lax.rem(seat, 2)
    bits = [lax.rem(lax.div(own, 2 ** (levels - 1 - level)), 2) for level in range(levels)]

    barrier = pltpu.get_barrier_semaphore()

    def greet(peer):
        pl.semaphore_signal(barrier, inc=1, device_id=peer, device_id_type=pl.DeviceIdType.MESH)

    greet({"ang": own ^ 1})
    greet({"tile": seat ^ 1})

    @pl.when(line > 0)
    def _():
        greet({"ang": own - 2})

    for step in range(1, lines):

        @pl.when(line + step < lines)
        def _():
            greet({"ang": own + 2 * step})

    loads = [
        pltpu.make_async_copy(sino_ref.at[core], field_in.at[own, :, pl.ds(0, bins)], in_sems.at[0]),
        pltpu.make_async_copy(offsets_ref, offsets, in_sems.at[1]),
    ]
    for level in range(levels):
        loads.append(pltpu.make_async_copy(merge_ref.at[level, bits[level]], merges.at[level], in_sems.at[2 + level]))
    for load in loads:
        load.start()
    loads[1].wait()
    place_code = lax.broadcasted_iota(jnp.int32, (angles, rows), 0) * (PITCH * LANES)
    codes = (jnp.bitwise_and(offsets[...] + (bins - 1), bins - 1) ^ (LANES - 1)) + place_code
    for part, (first, last) in enumerate(((0, cuts[0]), cuts, (cuts[1], rows))):
        index_in[own, :, pl.ds(part * LANES, last - first)] = codes[:, first:last]
    loads[0].wait()
    largest = jnp.max(jnp.abs(field_in[own, :, pl.ds(0, bins)]))
    field_in[own, :, pl.ds(bins, LANES)] = jnp.full((angles, LANES), 1.0, jnp.float32) * largest
    pl.semaphore_wait(barrier, 2 + line + jnp.where(line < lines - 1, 1, 0))

    def send(n, group, kind, slot, target):
        buffer = (index_in, field_in)[n]
        return pltpu.make_async_remote_copy(
            src_ref=buffer.at[group],
            dst_ref=buffer.at[group],
            send_sem=send_sems.at[n, kind, slot],
            recv_sem=recv_sems.at[n, group],
            device_id={"ang": target},
            device_id_type=pl.DeviceIdType.MESH,
        )

    def send_across(n, source):
        return send(n, 2 * source + column, 0, source, own ^ 1)

    def send_far(n, target):
        return send(n, own, 1, target, 2 * target + column)

    for target in range(lines - 2):

        @pl.when(target < line - 1)
        def _():
            pl.semaphore_signal(
                ready_sem, inc=1, device_id={"ang": 2 * target + column}, device_id_type=pl.DeviceIdType.MESH
            )

    for n in range(2):
        send_across(n, line).start()

        @pl.when(line < lines - 1)
        def _():
            send_far(n, line + 1).start()

        for target in range(lines - 1):

            @pl.when(target < line)
            def _():
                send_far(n, target).start()

    def send_late():
        @pl.when(lines - 2 - line > 0)
        def _():
            pl.semaphore_wait(ready_sem, lines - 2 - line)

        for n in range(2):
            for target in range(lines - 1, 1, -1):

                @pl.when(target > line + 1)
                def _():
                    send_far(n, target).start()

    edge = jnp.minimum(line, lines - 1 - line)

    def line_at(rank):
        inside = jnp.where(rank % 2 == 1, line - (rank + 1) // 2, line + rank // 2)
        outside = jnp.where(line < lines - 1 - line, rank, lines - 1 - rank)
        return jnp.where(rank <= 2 * edge, inside, outside)

    def source_at(place):
        rank = jnp.where(place < 2, 0, jnp.where(place <= lines, place - 1, place - lines))
        straight = jnp.logical_or(place == 0, jnp.logical_and(place >= 2, place <= lines))
        return line_at(rank), jnp.where(straight, column, 1 - column)

    def receive(n, place):
        source, side = source_at(place)
        group = 2 * source + side

        @pl.when(place > 0)
        def _():
            send(n, group, 0, 0, own ^ 1).wait_recv()

        @pl.when(jnp.logical_and(place >= 2, place <= lines))
        def _():
            send_across(n, source).start()

        return group

    def index_copies(group, side):
        outer = pl.multiple_of(bits[0] * (2 * LANES), LANES)
        for part, at in enumerate((LANES, outer)):
            yield pltpu.make_async_copy(
                index_in.at[group, :, pl.ds(at, LANES)], index_smem.at[side, part], smem_sems.at[side, part]
            )

    def prepare(group, side):
        peak = field_in[group, :, pl.ds(bins, LANES)]
        scale = TOP / jnp.maximum(peak, 1e-30)
        blocks = bins // LANES
        coded = []
        for block in range(blocks):
            value = field_in[group, :, pl.ds(block * LANES, LANES)]
            coded.append((value * scale + (TOP + 1.5)).astype(jnp.int32))
        for block in range(blocks):
            upper = jnp.left_shift(coded[(block + blocks // 2) % blocks] - int(TOP + 1), 16)
            packed = jnp.bitwise_or(upper, coded[block])
            for at in (block, block + blocks):
                if at < PITCH - 1:
                    table_ref[side, pl.ds(at, angles, stride=PITCH), :] = packed
        return peak * (1.0 / (TOP * math.sqrt(angles)))

    reverse_lane = LANES - 1 - lax.broadcasted_iota(jnp.int32, (SUBLANES, LANES), 1)
    samples_half = groups * width * ROW_PITCH

    middle = cuts[1] - cuts[0]

    def project(group, side, unit):
        start = (group ^ own) * (width * ROW_PITCH)
        for q in range(width):
            total = None
            upper = None
            for a in range(angles):
                code = index_smem[side, int(q >= middle), a, q if q < middle else q - middle]
                turn = jnp.bitwise_and(code, LANES - 1)
                base = jnp.right_shift(code, 7)
                near = table_ref[side, pl.ds(base, SUBLANES), :]
                next_ = table_ref[side, pl.ds(base + 1, SUBLANES), :]
                moved = pltpu.roll(jnp.where(reverse_lane < turn, near, next_), turn, 1)
                high = jnp.right_shift(moved, 16)
                total = moved if a == 0 else total + moved
                upper = high if a == 0 else upper + high
            lower = total - jnp.left_shift(upper, 16) - angles * int(TOP + 1)
            at = start + q * ROW_PITCH
            samples_ref[0, pl.ds(at, SUBLANES), :] = lower.astype(jnp.float32) * unit
            samples_ref[1, pl.ds(at, SUBLANES), :] = upper.astype(jnp.float32) * unit

    def prepare_weights():
        for load in loads[2:]:
            load.wait()
        parts = None
        for level in range(levels - 1, -1, -1):
            matrices = [merges[level, m] for m in range(2)]
            if level == 0:
                outer = [jnp.where(bits[0] == 1, m[:, cuts[1]:], m[:, : cuts[0]]) for m in matrices]
                matrices = [jnp.concatenate([m[:, cuts[0]:cuts[1]], o], axis=1) for m, o in zip(matrices, outer)]
            if parts is None:
                parts = matrices
            else:
                matrices = [split_bf16(m) for m in matrices]
                parts = [dot3(part, m) for part in [split_bf16(p) for p in parts] for m in matrices]
        flips = [int(format(k, f"0{levels}b")[::-1], 2) for k in range(groups)]
        whole = jnp.concatenate([parts[i] for i in flips], axis=1)
        weights_high[...], weights_low[...] = split_bf16(whole)

    for copy in index_copies(own, 0):
        copy.start()
    prepare_weights()

    def advance(place, side):
        last = place + 1 == groups

        @pl.when(place == 1)
        def _():
            send_late()
            for copy in index_copies(receive(0, place), side):
                copy.start()

        @pl.when(jnp.logical_and(place > 0, jnp.logical_not(last)))
        def _():
            for copy in index_copies(receive(0, place + 1), 1 - side):
                copy.start()

        group = receive(1, place)
        unit = prepare(group, side)
        for copy in index_copies(group, side):
            copy.wait()
        project(group, side, unit)

    def by_pairs(step, carry):
        advance(2 * step, 0)
        advance(2 * step + 1, 1)
        return carry

    lax.fori_loop(0, groups // 2, by_pairs, 0)

    depth = groups * width
    pairs = bins // (2 * LANES)

    def swap(n):
        at = pl.ds(pl.multiple_of(n * 2 * LANES, 2 * LANES), 2 * LANES)
        return pltpu.make_async_remote_copy(
            src_ref=out_ref.at[core, :, at],
            dst_ref=out_ref.at[core, :, at],
            send_sem=swap_send.at[n],
            recv_sem=swap_recv.at[n],
            device_id={"tile": seat ^ 1},
            device_id_type=pl.DeviceIdType.MESH,
        )

    def by_columns(n, carry):
        @pl.when(n > 0)
        def _():
            swap(n - 1).start()

        side = n // (pairs // 2)
        first = (n % (pairs // 2)) * 2
        parts = [samples_ref[side, pl.ds(first + i, depth, stride=ROW_PITCH), :] for i in range(2)]
        field = split_bf16(jnp.concatenate(parts, axis=1))
        total = dot3((weights_high[...], weights_low[...]), field)
        out_ref[core, :, pl.ds(pl.multiple_of(n * 2 * LANES, 2 * LANES), 2 * LANES)] = total
        return carry

    lax.fori_loop(0, pairs, by_columns, 0)
    swap(pairs - 1).start()
    for n in range(2):
        for source in range(lines):
            send_across(n, source).wait_send()

            @pl.when(source != line)
            def _():
                send_far(n, source).wait_send()

    for n in range(pairs):
        swap(n).wait()


def body(sinogram, ray_offsets, merge_matrices):
    slices, angles, bins = sinogram.shape
    rows = ray_offsets.shape[1]
    levels = merge_matrices.shape[0]
    groups = lax.axis_size("ang")
    assert slices == 2 and lax.axis_size("tile") % 2 == 0
    assert groups == 2**levels and angles == SUBLANES and bins == 2 * SUBLANES * LANES
    width = rows // 2 + rows // 8
    vmem = pl.BlockSpec(memory_space=pltpu.VMEM)
    hbm = pl.BlockSpec(memory_space=pltpu.HBM)
    dma = pltpu.SemaphoreType.DMA
    return pl.pallas_call(
        functools.partial(fused_kernel, (levels, angles, rows, bins)),
        out_shape=pltpu.VMEM((slices, rows, bins), jnp.float32),
        in_specs=[hbm, hbm, hbm],
        out_specs=vmem,
        scratch_shapes=[
            pltpu.VMEM((groups, angles, bins + LANES), jnp.float32),
            pltpu.VMEM((groups, angles, 3 * LANES), jnp.int32),
            pltpu.SMEM((2, 2, angles, LANES), jnp.int32),
            pltpu.VMEM((angles, rows), jnp.int32),
            pltpu.VMEM((levels, 2, rows, rows), jnp.float32),
            pltpu.VMEM((2, angles * PITCH, LANES), jnp.int32),
            pltpu.VMEM((2, groups * width * ROW_PITCH + SUBLANES, LANES), jnp.float32),
            pltpu.VMEM((rows, groups * width), jnp.bfloat16),
            pltpu.VMEM((rows, groups * width), jnp.bfloat16),
            dma((2 + levels,)),
            dma((2, 2)),
            dma((2, 2, groups // 2)),
            dma((2, groups)),
            pltpu.SemaphoreType.REGULAR,
            dma((bins // (2 * LANES),)),
            dma((bins // (2 * LANES),)),
        ],
        compiler_params=pltpu.CompilerParams(
            collective_id=0, has_side_effects=True, vmem_limit_bytes=48 * 1024 * 1024
        ),
    )(*[pltpu.with_memory_space_constraint(x, pltpu.HBM) for x in (sinogram, ray_offsets, merge_matrices)])


def solution(mesh):
    placed = (P(None, "ang", None), P("ang", None), P())
    return jax.shard_map(
        body, mesh=mesh, in_specs=placed, out_specs=P(None, "ang", None), check_vma=False
    )
```

time: 32.1 us -> 29.8 us (0.928)
  Pallas kernels: 29.9 us -> 27.7 us
    pallas_call x1, Pallas kernels: 29.9 us -> 27.7 us  [body(): pl.pallas_call(functools.partial(fused_kernel, (levels, angles, rows, bin...]
where the time goes in v3:
time: 29.8 us; the launch traced here: 29.7 us
  Pallas kernels  27.7 us (93%)
  local copies, waits for them, and re-layouts  2.02 us (7%)
    pallas_call x1, Pallas kernels, body(): pl.pallas_call(functools.partial(fused_kernel, (levels, angles, rows, bin...  27.7 us
    unnamed x1, local copies, waits for them, and re-layouts  2.02 us

profile of v3, /device:TPU:0, one launch (start us, length us, event | category | flops | bytes accessed | tf_op | source)
XLA Modules:
  0.0 29.7 jit_solution(1265392241341994914)
XLA Ops:
  0.0 27.7 %shard_map.37 = f32[2,256,2048]{2,1,0:T(8,128)S(1)} custom-call(f32[2,8,2048]{2,1,0:T(8,128)} %sino_ref.1, s32[8,256]{1,0:T(8,128)} %offsets_ref.1, f32[3,2,2,256,256]{4,3,2,1,0:T(8,128)} %merge_ref.1), custom_call_target="tpu_custom_call" | custom-call | tf_op jit(solution)/shard_map/pallas_call | solution.py:302
  27.7 2.0 %copy.5 = f32[2,256,2048]{2,1,0:T(8,128)} copy(f32[2,256,2048]{2,1,0:T(8,128)S(1)} %shard_map.37) | data formatting | bytes 8388608
